TPU v7x, 32 devices: a whole 2x2x4 slice. The times are simulated.
32 devices in a mesh: energy: 16 (over z, y, core), cuts: 2 (over x).
Axes of the slice: x: 2, y: 2, z: 4, core: 2. Of those that a mesh axis runs over, the one named last changes fastest.
Arguments:
- green: bfloat16 [64, 2, 4, 128, 128], P('energy', 'cuts'), may hold values from -6 to 6
- offsets: int32 [4], replicated, may hold values from 1 to 2
- occupation: float32 [4], replicated, may hold values from 0.05 to 2
- coupling: bfloat16 [4, 3, 2, 128, 128], P(None, None, 'cuts'), may hold values from -0.25 to 0.25
Outputs:
- sigma: float32 [64, 2, 4, 128, 128], P('energy', 'cuts')
All inputs are finite; a program needn't handle non-finite values.
Results may differ from a plain program's by a relative error of at most 0.0041.
Values may be sent and summed in bfloat16 or wider, within the bound.
A program may use at most 64 MiB of HBM per device.

v0:
```python
import functools
import jax
import jax.numpy as jnp
from jax import lax
from jax.experimental import pallas as pl
from jax.experimental.pallas import tpu as pltpu
from jax.sharding import PartitionSpec as P

OFFMAX = 2
MESH = pl.DeviceIdType.MESH


def kernel(n_energy, n_cuts, slots, offsets_in, occupation_in, green, coupling, acc,
           offsets, occupation, ext, kbuf, kt, small_sem, local_sem, k_sem,
           own_send, own_recv, x_send, x_recv, relay_send, relay_recv):
    rank = lax.axis_index("energy")
    cut = lax.axis_index("cuts")
    count, parts = ext.shape[2] - 2 * OFFMAX, ext.shape[1]
    branches, width = kbuf.shape[0], kbuf.shape[2]
    reach = OFFMAX
    first = rank % 2
    second = 1 - first

    def at(energy, slice_):
        return {"energy": energy, "cuts": slice_}

    has = (rank > 0, rank < n_energy - 1)
    beside = (jnp.maximum(rank - 1, 0), jnp.minimum(rank + 1, n_energy - 1))
    if slots == 1:
        partners = [(1, 1, 1 - cut, None, 2 - 2 * cut)]
    elif slots == 2:
        partners = [
            (1, 2, jnp.maximum(cut - 1, 0), cut > 0, 0),
            (2, 1, jnp.minimum(cut + 1, n_cuts - 1), cut < n_cuts - 1, 2),
        ]
    else:
        partners = []

    def when(cond, do):
        if cond is None:
            do()
        else:
            pl.when(cond)(do)

    def exists(p):
        return jnp.where(p == 0, rank, n_energy - 1 - rank) > 0

    def toward(p):
        return jnp.clip(rank + 2 * p - 1, 0, n_energy - 1)

    def source(p):
        return (count - reach) * p + reach

    def landing(p):
        return (count + reach) * (1 - p)

    def own_copy(p, c):
        return pltpu.make_async_remote_copy(
            src_ref=ext.at[0, c, pl.ds(source(p), reach)],
            dst_ref=ext.at[0, c, pl.ds(landing(p), reach)],
            send_sem=own_send.at[p, c], recv_sem=own_recv.at[p, c],
            device_id=at(toward(p), cut), device_id_type=MESH)

    def relay_copy(slot, p, c):
        return pltpu.make_async_remote_copy(
            src_ref=ext.at[slot, c, pl.ds(source(p), reach)],
            dst_ref=ext.at[slot, c, pl.ds(landing(p), reach)],
            send_sem=relay_send.at[slot - 1, p, c], recv_sem=relay_recv.at[slot - 1, p, c],
            device_id=at(toward(p), cut), device_id_type=MESH)

    def x_copy(there, partner, p, c):
        return pltpu.make_async_remote_copy(
            src_ref=ext.at[0, c, pl.ds(source(p), reach)],
            dst_ref=ext.at[there, c, pl.ds(source(p), reach)],
            send_sem=x_send.at[there - 1, p, c], recv_sem=x_recv.at[there - 1, p, c],
            device_id=at(rank, partner), device_id_type=MESH)

    barrier = pltpu.get_barrier_semaphore()
    for p in range(2):
        pl.when(has[p])(functools.partial(
            pl.semaphore_signal, barrier, inc=1, device_id=at(beside[p], cut), device_id_type=MESH))
    for here, there, partner, cond, side in partners:
        when(cond, functools.partial(
            pl.semaphore_signal, barrier, inc=1, device_id=at(rank, partner), device_id_type=MESH))

    local = [pltpu.make_async_copy(green.at[:, 0, c], ext.at[0, c, pl.ds(reach, count)], local_sem.at[c])
             for c in range(parts)]
    for c in range(parts):
        local[c].start()
    k_copy = pltpu.make_async_copy(coupling.at[:, :, 0], kbuf, k_sem)
    k_copy.start()
    small = [pltpu.make_async_copy(offsets_in, offsets, small_sem.at[0]),
             pltpu.make_async_copy(occupation_in, occupation, small_sem.at[1])]
    for copy in small:
        copy.start()

    peers = sum(flag.astype(jnp.int32) for flag in has)
    for here, there, partner, cond, side in partners:
        peers = peers + (1 if cond is None else cond.astype(jnp.int32))
    pl.semaphore_wait(barrier, peers)

    order = [(0, 0)]
    for c in range(1, parts):
        order += [(0, c), (1, c - 1)]
    order += [(1, parts - 1)]
    waited = set()
    for which, c in order:
        if c not in waited:
            local[c].wait()
            waited.add(c)
        p = (first, second)[which]
        for here, there, partner, cond, side in partners:
            when(cond, lambda: x_copy(there, partner, p, c).start())
        if which == 0:
            for q in (first, second):
                pl.when(exists(q))(lambda: own_copy(q, c).start())

    @pl.when(rank == 0)
    def _():
        ext[:, :, pl.ds(0, reach)] = jnp.zeros((slots + 1, parts, reach, width, width), ext.dtype)

    @pl.when(rank == n_energy - 1)
    def _():
        ext[:, :, pl.ds(count + reach, reach)] = jnp.zeros((slots + 1, parts, reach, width, width), ext.dtype)

    k_copy.wait()
    for copy in small:
        copy.wait()
    for s in range(kbuf.shape[1]):
        for b in range(branches):
            kt[s, b * width:(b + 1) * width, :] = kbuf[b, s].T

    def forward(which, c):
        p = (first, second)[which]
        for here, there, partner, cond, side in partners:
            def go():
                x_copy(here, partner, p, c).wait_recv()
                pl.when(exists(p))(lambda: relay_copy(here, p, c).start())
            when(cond, go)

    def own_ready(c):
        for p in range(2):
            pl.when(has[p])(lambda: own_copy(1 - p, c).wait_recv())

    steps = parts * (slots + 1)
    last = 2 * parts - 2
    plan = {}
    for position, item in enumerate(order if partners else []):
        plan.setdefault(min(position, last), []).append(item)

    def compute(slot, side, c):
        values = [ext[slot, c, e].astype(jnp.float32) for e in range(count + 2 * reach)]
        lefts = []
        for b in range(branches):
            n = occupation[b]
            w = offsets[b]
            lesser = c < parts // 2
            lower = jnp.where(lesser, n, n + 1.0)
            upper = jnp.where(lesser, n + 1.0, n)
            low = [jnp.where(w == d, lower, 0.0) for d in range(1, reach + 1)]
            up = [jnp.where(w == d, upper, 0.0) for d in range(1, reach + 1)]
            mixed = []
            for e in range(count):
                total = None
                for d in range(1, reach + 1):
                    term = low[d - 1] * values[reach + e - d] + up[d - 1] * values[reach + e + d]
                    total = term if total is None else total + term
                mixed.append(total.astype(jnp.bfloat16))
            lefts.append(jnp.dot(kbuf[b, side], jnp.concatenate(mixed, axis=1),
                                 preferred_element_type=jnp.float32).astype(jnp.bfloat16))
        rows = [jnp.concatenate([left[:, e * width:(e + 1) * width] for left in lefts], axis=1)
                for e in range(count)]
        return jnp.dot(jnp.concatenate(rows, axis=0), kt[side], preferred_element_type=jnp.float32)

    def step(t, carry):
        slot = t // parts
        c = t % parts
        for k, todo in plan.items():
            @pl.when(t == k)
            def _():
                for which, part in todo:
                    forward(which, part)

        @pl.when(slot == 0)
        def _():
            own_ready(c)

        runs = slot == 0
        side = jnp.where(slot == 0, 1, 0)
        for here, there, partner, cond, which_side in partners:
            side = jnp.where(slot == here, which_side, side)
            mine = slot == here
            if cond is not None:
                mine = jnp.logical_and(mine, cond)
            runs = jnp.logical_or(runs, mine)

            @pl.when(mine)
            def _():
                for p in range(2):
                    pl.when(has[p])(lambda: relay_copy(here, 1 - p, c).wait_recv())

        def work():
            sums = compute(slot, side, c)

            @pl.when(slot == 0)
            def _():
                for e in range(count):
                    acc[c, e] = sums[e * width:(e + 1) * width]

            @pl.when(slot > 0)
            def _():
                for e in range(count):
                    acc[c, e] += sums[e * width:(e + 1) * width]

        if slots == 2:
            pl.when(runs)(work)
        else:
            work()

        return carry

    lax.fori_loop(0, steps, step, 0)

    for c in range(parts):
        for p in range(2):
            pl.when(has[p])(lambda: own_copy(p, c).wait_send())
            for here, there, partner, cond, side in partners:
                when(cond, lambda: x_copy(there, partner, p, c).wait_send())
                both = has[p] if cond is None else jnp.logical_and(cond, has[p])
                pl.when(both)(lambda: relay_copy(here, p, c).wait_send())


def write_out(sums, out, sem):
    copies = [pltpu.make_async_copy(sums.at[c], out.at[:, 0, c], sem.at[c]) for c in range(sums.shape[0])]
    for copy in copies:
        copy.start()
    for copy in copies:
        copy.wait()


def body(n_energy, n_cuts, green, offsets, occupation, coupling):
    count, slices, parts, width, _ = green.shape
    branches, sides = coupling.shape[:2]
    assert slices == 1 and count == 2 * OFFMAX
    slots = min(n_cuts - 1, 2)
    sems = max(slots, 1)
    dma = pltpu.SemaphoreType.DMA
    sums = pl.pallas_call(
        functools.partial(kernel, n_energy, n_cuts, slots),
        out_shape=pltpu.VMEM((parts, count, width, width), jnp.float32),
        in_specs=[
            pl.BlockSpec(memory_space=pl.ANY),
            pl.BlockSpec(memory_space=pl.ANY),
            pl.BlockSpec(memory_space=pl.ANY),
            pl.BlockSpec(memory_space=pl.ANY),
        ],
        out_specs=pl.BlockSpec(memory_space=pltpu.VMEM),
        scratch_shapes=[
            pltpu.SMEM(offsets.shape, offsets.dtype),
            pltpu.SMEM(occupation.shape, occupation.dtype),
            pltpu.VMEM((slots + 1, parts, count + 2 * OFFMAX, width, width), jnp.bfloat16),
            pltpu.VMEM((branches, sides, width, width), jnp.bfloat16),
            pltpu.VMEM((sides, branches * width, width), jnp.bfloat16),
            dma((2,)),
            dma((parts,)),
            dma,
            dma((2, parts)),
            dma((2, parts)),
            dma((sems, 2, parts)),
            dma((sems, 2, parts)),
            dma((sems, 2, parts)),
            dma((sems, 2, parts)),
        ],
        compiler_params=pltpu.CompilerParams(collective_id=0, has_side_effects=True),
    )(offsets, occupation, green, coupling)
    return pl.pallas_call(
        write_out,
        out_shape=jax.ShapeDtypeStruct(green.shape, jnp.float32),
        in_specs=[pl.BlockSpec(memory_space=pltpu.VMEM)],
        out_specs=pl.BlockSpec(memory_space=pl.ANY),
        scratch_shapes=[dma((parts,))],
    )(pltpu.with_memory_space_constraint(sums, pltpu.VMEM))


def solution(mesh):
    sizes = dict(mesh.shape)
    in_specs = (P("energy", "cuts", None, None, None), P(), P(), P(None, None, "cuts", None, None))
    out_specs = P("energy", "cuts", None, None, None)
    return jax.shard_map(
        functools.partial(body, sizes["energy"], sizes["cuts"]),
        mesh=mesh, in_specs=in_specs, out_specs=out_specs, check_vma=False)
```

profile of v0, /device:TPU:0, one launch (start us, length us, event | category | flops | bytes accessed | tf_op | source)
XLA Modules:
  0.0 19.6 jit_solution(7422022101305235997)
XLA Ops:
  0.0 18.6 %shard_map.46.sums = f32[4,4,128,128]{3,2,1,0:T(8,128)S(1)} custom-call(s32[4]{0:T(128)} %offsets_in.1, f32[4]{0:T(128)} %occupation_in.1, bf16[4,1,4,128,128]{4,3,2,1,0:T(8,128)(2,1)} %green.1, bf16[4,3,1,128,128]{4,3,2,1,0:T(8,128)(2,1)} %coupling.1), custom_call_target="tpu_custom_call" | custom-call | tf_op jit(solution)/shard_map/pallas_call | solution.py:248
  18.6 1.0 %shard_map.47 = f32[4,1,4,128,128]{4,3,2,1,0:T(8,128)} custom-call(f32[4,4,128,128]{3,2,1,0:T(8,128)S(1)} %shard_map.46.sums), custom_call_target="tpu_custom_call" | custom-call | tf_op jit(solution)/shard_map/pallas_call | solution.py:276
where the time goes:
time: 19.8 us; the launch traced here: 19.6 us
  Pallas kernels  19.6 us (99%)
    pallas_call x1, Pallas kernels, body(): pl.pallas_call(functools.partial(kernel, n_energy, n_cuts, slots), out_sh...  18.6 us
    pallas_call x1, Pallas kernels, body(): pl.pallas_call(write_out, out_shape=jax.ShapeDtypeStruct(green.shape, jnp...  1 us

commit v1 on v0

--- a/solution.py
+++ b/solution.py
@@ -54,9 +54,12 @@
     def landing(p):
         return (count + reach) * (1 - p)
 
+    def edge(p, c):
+        return green.at[pl.ds((count - reach) * p, reach), 0, c]
+
     def own_copy(p, c):
         return pltpu.make_async_remote_copy(
-            src_ref=ext.at[0, c, pl.ds(source(p), reach)],
+            src_ref=edge(p, c),
             dst_ref=ext.at[0, c, pl.ds(landing(p), reach)],
             send_sem=own_send.at[p, c], recv_sem=own_recv.at[p, c],
             device_id=at(toward(p), cut), device_id_type=MESH)
@@ -70,7 +73,7 @@
 
     def x_copy(there, partner, p, c):
         return pltpu.make_async_remote_copy(
-            src_ref=ext.at[0, c, pl.ds(source(p), reach)],
+            src_ref=edge(p, c),
             dst_ref=ext.at[there, c, pl.ds(source(p), reach)],
             send_sem=x_send.at[there - 1, p, c], recv_sem=x_recv.at[there - 1, p, c],
             device_id=at(rank, partner), device_id_type=MESH)
@@ -103,11 +106,7 @@
     for c in range(1, parts):
         order += [(0, c), (1, c - 1)]
     order += [(1, parts - 1)]
-    waited = set()
     for which, c in order:
-        if c not in waited:
-            local[c].wait()
-            waited.add(c)
         p = (first, second)[which]
         for here, there, partner, cond, side in partners:
             when(cond, lambda: x_copy(there, partner, p, c).start())
@@ -124,7 +123,7 @@
         ext[:, :, pl.ds(count + reach, reach)] = jnp.zeros((slots + 1, parts, reach, width, width), ext.dtype)
 
     k_copy.wait()
-    for copy in small:
+    for copy in small + local:
         copy.wait()
     for s in range(kbuf.shape[1]):
         for b in range(branches):

time: 19.8 us -> 19.1 us (0.965)
  Pallas kernels: 19.6 us -> 18.9 us
    pallas_call x1, Pallas kernels: 18.6 us -> 17.9 us  [body(): pl.pallas_call(functools.partial(kernel, n_energy, n_cuts, slots), out_sh...]
where the time goes in v1:
time: 19.1 us; the launch traced here: 18.9 us
  Pallas kernels  18.9 us (99%)
    pallas_call x1, Pallas kernels, body(): pl.pallas_call(functools.partial(kernel, n_energy, n_cuts, slots), out_sh...  17.9 us
    pallas_call x1, Pallas kernels, body(): pl.pallas_call(write_out, out_shape=jax.ShapeDtypeStruct(green.shape, jnp...  1 us

profile of v1, /device:TPU:0, one launch (start us, length us, event | category | flops | bytes accessed | tf_op | source)
XLA Modules:
  0.0 18.9 jit_solution(11272274519286931842)
XLA Ops:
  0.0 17.9 %shard_map.46.sums = f32[4,4,128,128]{3,2,1,0:T(8,128)S(1)} custom-call(s32[4]{0:T(128)} %offsets_in.1, f32[4]{0:T(128)} %occupation_in.1, bf16[4,1,4,128,128]{4,3,2,1,0:T(8,128)(2,1)} %green.1, bf16[4,3,1,128,128]{4,3,2,1,0:T(8,128)(2,1)} %coupling.1), custom_call_target="tpu_custom_call" | custom-call | tf_op jit(solution)/shard_map/pallas_call | solution.py:247
  17.9 1.0 %shard_map.47 = f32[4,1,4,128,128]{4,3,2,1,0:T(8,128)} custom-call(f32[4,4,128,128]{3,2,1,0:T(8,128)S(1)} %shard_map.46.sums), custom_call_target="tpu_custom_call" | custom-call | tf_op jit(solution)/shard_map/pallas_call | solution.py:275

commit v2 on v1

--- a/solution.py
+++ b/solution.py
@@ -281,10 +281,275 @@
     )(pltpu.with_memory_space_constraint(sums, pltpu.VMEM))
 
 
+def pair_kernel(n_energy, offsets_in, occupation_in, green, coupling, acc,
+                offsets, occupation, ext, kbuf, kt, edge_out, edge_in, local_sem,
+                reply_x, reply_e, send, x_recv, own_recv, relay_recv, edge_recv):
+    rank = lax.axis_index("energy")
+    cut = lax.axis_index("cuts")
+    reach = OFFMAX
+    count, parts, width = ext.shape[1] - 2 * reach, ext.shape[2], ext.shape[3]
+    branches = kbuf.shape[1]
+    outer = rank % 2
+    inner = 1 - outer
+    has_outer = jnp.where(outer == 0, rank, n_energy - 1 - rank) > 0
+    early = jnp.where(has_outer, outer, inner)
+    late = 1 - early
+    core_peer = {"energy": rank + 1 - 2 * outer, "cuts": cut}
+    chip_peer = {"energy": jnp.clip(rank - 1 + 2 * outer, 0, n_energy - 1), "cuts": cut}
+    slice_peer = {"energy": rank, "cuts": 1 - cut}
+    told = (rank + cut) % 2 == 1
+    tells = (rank + cut) % 2 == 0
+
+    def own_at(p):
+        return pl.ds(reach + (count - reach) * p, reach)
+
+    def halo_at(p):
+        return pl.ds((count + reach) * p, reach)
+
+    def edge_at(p):
+        return pl.ds((count - reach) * p, reach)
+
+    def x_copy(p, c):
+        return pltpu.make_async_remote_copy(
+            src_ref=green.at[edge_at(p), 0, c], dst_ref=ext.at[1, own_at(p), c],
+            send_sem=send.at[0], recv_sem=x_recv.at[p, c], device_id=slice_peer, device_id_type=MESH)
+
+    def own_copy():
+        return pltpu.make_async_remote_copy(
+            src_ref=green.at[edge_at(inner), 0], dst_ref=ext.at[0, halo_at(outer)],
+            send_sem=send.at[1], recv_sem=own_recv, device_id=core_peer, device_id_type=MESH)
+
+    def relay_copy(c):
+        return pltpu.make_async_remote_copy(
+            src_ref=ext.at[1, own_at(inner), c], dst_ref=ext.at[1, halo_at(outer), c],
+            send_sem=send.at[2], recv_sem=relay_recv.at[c], device_id=core_peer, device_id_type=MESH)
+
+    def edge_copy(c):
+        return pltpu.make_async_remote_copy(
+            src_ref=edge_out.at[c], dst_ref=edge_in.at[c],
+            send_sem=send.at[3], recv_sem=edge_recv.at[c], device_id=chip_peer, device_id_type=MESH)
+
+    def signal(sem, device):
+        pl.semaphore_signal(sem, inc=1, device_id=device, device_id_type=MESH)
+
+    barrier = pltpu.get_barrier_semaphore()
+
+    @pl.when(tells)
+    def _():
+        signal(barrier, slice_peer)
+
+    @pl.when(told)
+    def _():
+        signal(barrier, core_peer)
+
+    @pl.when(jnp.logical_and(told, has_outer))
+    def _():
+        signal(barrier, chip_peer)
+
+    @pl.when(told)
+    def _():
+        pl.semaphore_wait(barrier, 1)
+        signal(reply_x, slice_peer)
+
+    @pl.when(tells)
+    def _():
+        pl.semaphore_wait(reply_x, 1)
+
+    for p in (early, late):
+        for c in range(parts):
+            x_copy(p, c).start()
+
+    local = [pltpu.make_async_copy(green.at[:, 0], ext.at[0, pl.ds(reach, count)], local_sem.at[0]),
+             pltpu.make_async_copy(coupling.at[:, 1, 0], kbuf.at[0], local_sem.at[1]),
+             pltpu.make_async_copy(coupling.at[:, 2 - 2 * cut, 0], kbuf.at[1], local_sem.at[2]),
+             pltpu.make_async_copy(offsets_in, offsets, local_sem.at[3]),
+             pltpu.make_async_copy(occupation_in, occupation, local_sem.at[4])]
+    for copy in local:
+        copy.start()
+
+    @pl.when(tells)
+    def _():
+        pl.semaphore_wait(barrier, 1 + has_outer.astype(jnp.int32))
+        signal(reply_e.at[0], core_peer)
+
+    @pl.when(jnp.logical_and(tells, has_outer))
+    def _():
+        signal(reply_e.at[1], chip_peer)
+
+    @pl.when(told)
+    def _():
+        pl.semaphore_wait(reply_e.at[0], 1)
+
+    own_copy().start()
+
+    ext[:, halo_at(outer)] = jnp.zeros((2, reach, parts, width, width), ext.dtype)
+    for copy in local:
+        copy.wait()
+    for s in range(2):
+        for b in range(branches):
+            kt[s, b * width:(b + 1) * width, :] = kbuf[s, b].T
+
+    @pl.when(jnp.logical_and(told, has_outer))
+    def _():
+        pl.semaphore_wait(reply_e.at[1], 1)
+
+    own_copy().wait_recv()
+
+    def weights(c):
+        lesser = c < parts // 2
+        lower = [jnp.where(lesser, occupation[b], occupation[b] + 1.0) for b in range(branches)]
+        upper = [jnp.where(lesser, occupation[b] + 1.0, occupation[b]) for b in range(branches)]
+        return lower, upper, [offsets[b] == 1 for b in range(branches)]
+
+    def unit(s, c):
+        lower, upper, near = weights(c)
+        values = [ext[s, e, c].astype(jnp.float32) for e in range(count + 2 * reach)]
+        lefts = []
+        for b in range(branches):
+            mixed = []
+            for e in range(reach, reach + count):
+                below = jnp.where(near[b], values[e - 1], values[e - 2])
+                above = jnp.where(near[b], values[e + 1], values[e + 2])
+                mixed.append((lower[b] * below + upper[b] * above).astype(jnp.bfloat16))
+            lefts.append(jnp.dot(kbuf[s, b], jnp.concatenate(mixed, axis=1),
+                                 preferred_element_type=jnp.float32).astype(jnp.bfloat16))
+        rows = [jnp.concatenate([left[:, e * width:(e + 1) * width] for left in lefts], axis=1)
+                for e in range(count)]
+        return jnp.dot(jnp.concatenate(rows, axis=0), kt[s], preferred_element_type=jnp.float32)
+
+    def edge(c):
+        lower, upper, near = weights(c)
+        lefts = []
+        for s in range(2):
+            first = ext[s, reach + (count - 1) * outer, c].astype(jnp.float32)
+            second = ext[s, reach + 1 + (count - 3) * outer, c].astype(jnp.float32)
+            for b in range(branches):
+                gain = jnp.where(outer == 0, upper[b], lower[b])
+                one = gain * jnp.where(near[b], first, second)
+                two = jnp.where(near[b], 0.0, gain) * first
+                both = jnp.concatenate([one.astype(jnp.bfloat16), two.astype(jnp.bfloat16)], axis=1)
+                lefts.append(jnp.dot(kbuf[s, b], both, preferred_element_type=jnp.float32).astype(jnp.bfloat16))
+        rows = [jnp.concatenate([left[:, e * width:(e + 1) * width] for left in lefts], axis=1)
+                for e in range(reach)]
+        sums = jnp.dot(jnp.concatenate(rows, axis=0), kt[...].reshape(2 * branches * width, width),
+                       preferred_element_type=jnp.float32).astype(edge_out.dtype)
+        for e in range(reach):
+            edge_out[c, e] = sums[e * width:(e + 1) * width]
+
+    def first_half(c, carry):
+        sums = unit(0, c)
+        for e in range(count):
+            acc[e, c] = sums[e * width:(e + 1) * width]
+
+        @pl.when(jnp.logical_and(has_outer, c > 0))
+        def _():
+            edge_copy(c - 1).start()
+
+        x_copy(early, c).wait_recv()
+
+        @pl.when(has_outer)
+        def _():
+            edge(c)
+
+        @pl.when(jnp.logical_not(has_outer))
+        def _():
+            relay_copy(c).start()
+
+        return carry
+
+    lax.fori_loop(0, parts, first_half, 0)
+
+    def second_half(t, carry):
+        @pl.when(t < parts)
+        def _():
+            x_copy(late, t).wait_recv()
+            pl.when(has_outer)(lambda: relay_copy(t).start())
+
+        @pl.when(jnp.logical_and(has_outer, t == 0))
+        def _():
+            edge_copy(parts - 1).start()
+
+        @pl.when(t > 0)
+        def _():
+            c = t - 1
+            relay_copy(c).wait_recv()
+            sums = unit(1, c)
+            for e in range(count):
+                acc[e, c] += sums[e * width:(e + 1) * width]
+
+            @pl.when(has_outer)
+            def _():
+                edge_copy(c).wait_recv()
+                acc[(count - 1) * outer, c] += edge_in[c, 0].astype(jnp.float32)
+                acc[1 + (count - 3) * outer, c] += edge_in[c, 1].astype(jnp.float32)
+
+        return carry
+
+    lax.fori_loop(0, parts + 1, second_half, 0)
+
+    def sent(ref, n):
+        pltpu.make_async_copy(ref, ref, send.at[n]).wait()
+
+    sent(ext.at[1, pl.ds(reach, count)], 0)
+    sent(ext.at[0, pl.ds(0, reach)], 1)
+    sent(ext.at[1, pl.ds(0, reach)], 2)
+    pl.when(has_outer)(lambda: sent(edge_out, 3))
+
+
+def pair_write(sums, out, sem):
+    parts = sums.shape[1]
+    copies = [pltpu.make_async_copy(sums.at[:, c], out.at[:, 0, c], sem.at[c]) for c in range(parts)]
+    for copy in copies:
+        copy.start()
+    for copy in copies:
+        copy.wait()
+
+
+def pair_body(n_energy, green, offsets, occupation, coupling):
+    count, slices, parts, width, _ = green.shape
+    branches = coupling.shape[0]
+    assert slices == 1 and count == 2 * OFFMAX
+    dma = pltpu.SemaphoreType.DMA
+    regular = pltpu.SemaphoreType.REGULAR
+    sums = pl.pallas_call(
+        functools.partial(pair_kernel, n_energy),
+        out_shape=pltpu.VMEM((count, parts, width, width), jnp.float32),
+        in_specs=[pl.BlockSpec(memory_space=pl.ANY)] * 4,
+        out_specs=pl.BlockSpec(memory_space=pltpu.VMEM),
+        scratch_shapes=[
+            pltpu.SMEM(offsets.shape, offsets.dtype),
+            pltpu.SMEM(occupation.shape, occupation.dtype),
+            pltpu.VMEM((2, count + 2 * OFFMAX, parts, width, width), jnp.bfloat16),
+            pltpu.VMEM((2, branches, width, width), jnp.bfloat16),
+            pltpu.VMEM((2, branches * width, width), jnp.bfloat16),
+            pltpu.VMEM((parts, OFFMAX, width, width), jnp.bfloat16),
+            pltpu.VMEM((parts, OFFMAX, width, width), jnp.bfloat16),
+            dma((5,)),
+            regular,
+            regular((2,)),
+            dma((4,)),
+            dma((2, parts)),
+            dma,
+            dma((parts,)),
+            dma((parts,)),
+        ],
+        compiler_params=pltpu.CompilerParams(collective_id=0, has_side_effects=True),
+    )(offsets, occupation, green, coupling)
+    return pl.pallas_call(
+        pair_write,
+        out_shape=jax.ShapeDtypeStruct(green.shape, jnp.float32),
+        in_specs=[pl.BlockSpec(memory_space=pltpu.VMEM)],
+        out_specs=pl.BlockSpec(memory_space=pl.ANY),
+        scratch_shapes=[dma((parts,))],
+    )(pltpu.with_memory_space_constraint(sums, pltpu.VMEM))
+
+
 def solution(mesh):
     sizes = dict(mesh.shape)
     in_specs = (P("energy", "cuts", None, None, None), P(), P(), P(None, None, "cuts", None, None))
     out_specs = P("energy", "cuts", None, None, None)
-    return jax.shard_map(
-        functools.partial(body, sizes["energy"], sizes["cuts"]),
-        mesh=mesh, in_specs=in_specs, out_specs=out_specs, check_vma=False)
+    if sizes["cuts"] == 2 and sizes["energy"] % 2 == 0:
+        step = functools.partial(pair_body, sizes["energy"])
+    else:
+        step = functools.partial(body, sizes["energy"], sizes["cuts"])
+    return jax.shard_map(step, mesh=mesh, in_specs=in_specs, out_specs=out_specs, check_vma=False)

time: 19.1 us -> 18.6 us (0.974)
  Pallas kernels: 18.9 us -> 18.4 us
    pallas_call x2, Pallas kernels: 18.9 us -> 18.4 us  [the longest x1 17.4 us: pair_body(): pl.pallas_call(functools.partial(pair_kernel, n_energy), out_shape=pltpu....]
where the time goes in v2:
time: 18.6 us; the launch traced here: 18.4 us
  Pallas kernels  18.4 us (99%)
    pallas_call x1, Pallas kernels, pair_body(): pl.pallas_call(functools.partial(pair_kernel, n_energy), out_shape=pltpu....  17.4 us
    pallas_call x1, Pallas kernels, pair_body(): pl.pallas_call(pair_write, out_shape=jax.ShapeDtypeStruct(green.shape, jn...  1 us

profile of v2, /device:TPU:0, one launch (start us, length us, event | category | flops | bytes accessed | tf_op | source)
XLA Modules:
  0.0 18.4 jit_solution(12682235853902238349)
XLA Ops:
  0.0 17.4 %shard_map.46.sums = f32[4,4,128,128]{3,2,1,0:T(8,128)S(1)} custom-call(s32[4]{0:T(128)} %offsets_in.1, f32[4]{0:T(128)} %occupation_in.1, bf16[4,1,4,128,128]{4,3,2,1,0:T(8,128)(2,1)} %green.1, bf16[4,3,1,128,128]{4,3,2,1,0:T(8,128)(2,1)} %coupling.1), custom_call_target="tpu_custom_call" | custom-call | tf_op jit(solution)/shard_map/pallas_call | solution.py:514
  17.4 1.0 %shard_map.47 = f32[4,1,4,128,128]{4,3,2,1,0:T(8,128)} custom-call(f32[4,4,128,128]{3,2,1,0:T(8,128)S(1)} %shard_map.46.sums), custom_call_target="tpu_custom_call" | custom-call | tf_op jit(solution)/shard_map/pallas_call | solution.py:538

commit v3 on v2

--- a/solution.py
+++ b/solution.py
@@ -7,6 +7,7 @@
 from jax.sharding import PartitionSpec as P
 
 OFFMAX = 2
+HOLD = ((3, 3, 4, 4), (2, 2, 3, 3))
 MESH = pl.DeviceIdType.MESH
 
 
@@ -281,13 +282,29 @@
     )(pltpu.with_memory_space_constraint(sums, pltpu.VMEM))
 
 
-def pair_kernel(n_energy, offsets_in, occupation_in, green, coupling, acc,
-                offsets, occupation, ext, kbuf, kt, edge_out, edge_in, local_sem,
+def targets(values, k, k_t, lower, upper, near):
+    width, reach = k_t.shape[1], OFFMAX
+    count = len(values) - 2 * reach
+    lefts = []
+    for b in range(k.shape[0]):
+        mixed = []
+        for e in range(reach, reach + count):
+            below = jnp.where(near[b], values[e - 1], values[e - 2])
+            above = jnp.where(near[b], values[e + 1], values[e + 2])
+            mixed.append((lower[b] * below + upper[b] * above).astype(jnp.bfloat16))
+        lefts.append(jnp.dot(k[b], jnp.concatenate(mixed, axis=1),
+                             preferred_element_type=jnp.float32).astype(jnp.bfloat16))
+    return [jnp.dot(jnp.concatenate([left[:, e * width:(e + 1) * width] for left in lefts], axis=1), k_t[...],
+                    preferred_element_type=jnp.float32) for e in range(count)]
+
+
+def pair_kernel(n_energy, offsets_in, occupation_in, green, coupling, acc, far, kbuf, kt, scales,
+                offsets, occupation, own, edge_out, edge_in, local_sem,
                 reply_x, reply_e, send, x_recv, own_recv, relay_recv, edge_recv):
     rank = lax.axis_index("energy")
     cut = lax.axis_index("cuts")
     reach = OFFMAX
-    count, parts, width = ext.shape[1] - 2 * reach, ext.shape[2], ext.shape[3]
+    count, parts, width = own.shape[0] - 2 * reach, own.shape[1], own.shape[2]
     branches = kbuf.shape[1]
     outer = rank % 2
     inner = 1 - outer
@@ -297,8 +314,8 @@
     core_peer = {"energy": rank + 1 - 2 * outer, "cuts": cut}
     chip_peer = {"energy": jnp.clip(rank - 1 + 2 * outer, 0, n_energy - 1), "cuts": cut}
     slice_peer = {"energy": rank, "cuts": 1 - cut}
-    told = (rank + cut) % 2 == 1
-    tells = (rank + cut) % 2 == 0
+    told = (rank + cut) % 2 == 0
+    tells = (rank + cut) % 2 == 1
 
     def own_at(p):
         return pl.ds(reach + (count - reach) * p, reach)
@@ -311,17 +328,17 @@
 
     def x_copy(p, c):
         return pltpu.make_async_remote_copy(
-            src_ref=green.at[edge_at(p), 0, c], dst_ref=ext.at[1, own_at(p), c],
+            src_ref=green.at[edge_at(p), 0, c], dst_ref=far.at[own_at(p), c],
             send_sem=send.at[0], recv_sem=x_recv.at[p, c], device_id=slice_peer, device_id_type=MESH)
 
     def own_copy():
         return pltpu.make_async_remote_copy(
-            src_ref=green.at[edge_at(inner), 0], dst_ref=ext.at[0, halo_at(outer)],
+            src_ref=green.at[edge_at(inner), 0], dst_ref=own.at[halo_at(outer)],
             send_sem=send.at[1], recv_sem=own_recv, device_id=core_peer, device_id_type=MESH)
 
     def relay_copy(c):
         return pltpu.make_async_remote_copy(
-            src_ref=ext.at[1, own_at(inner), c], dst_ref=ext.at[1, halo_at(outer), c],
+            src_ref=far.at[own_at(inner), c], dst_ref=far.at[halo_at(outer), c],
             send_sem=send.at[2], recv_sem=relay_recv.at[c], device_id=core_peer, device_id_type=MESH)
 
     def edge_copy(c):
@@ -355,11 +372,22 @@
     def _():
         pl.semaphore_wait(reply_x, 1)
 
-    for p in (early, late):
+    held_back = jnp.logical_and(outer == 1, rank > 1)
+    longer = jnp.logical_and(cut == 0, has_outer)
+    for c in range(parts):
+        x_copy(early, c).start()
+
+    @pl.when(jnp.logical_not(held_back))
+    def _():
         for c in range(parts):
-            x_copy(p, c).start()
-
-    local = [pltpu.make_async_copy(green.at[:, 0], ext.at[0, pl.ds(reach, count)], local_sem.at[0]),
+            x_copy(late, c).start()
+
+    def release(point):
+        for c in range(parts):
+            at = jnp.where(longer, HOLD[0][c], HOLD[1][c])
+            pl.when(jnp.logical_and(held_back, point == at))(lambda: x_copy(late, c).start())
+
+    local = [pltpu.make_async_copy(green.at[:, 0], own.at[pl.ds(reach, count)], local_sem.at[0]),
              pltpu.make_async_copy(coupling.at[:, 1, 0], kbuf.at[0], local_sem.at[1]),
              pltpu.make_async_copy(coupling.at[:, 2 - 2 * cut, 0], kbuf.at[1], local_sem.at[2]),
              pltpu.make_async_copy(offsets_in, offsets, local_sem.at[3]),
@@ -382,7 +410,8 @@
 
     own_copy().start()
 
-    ext[:, halo_at(outer)] = jnp.zeros((2, reach, parts, width, width), ext.dtype)
+    own[halo_at(outer)] = jnp.zeros((reach, parts, width, width), own.dtype)
+    far[halo_at(outer)] = jnp.zeros((reach, parts, width, width), far.dtype)
     for copy in local:
         copy.wait()
     for s in range(2):
@@ -401,28 +430,16 @@
         upper = [jnp.where(lesser, occupation[b] + 1.0, occupation[b]) for b in range(branches)]
         return lower, upper, [offsets[b] == 1 for b in range(branches)]
 
-    def unit(s, c):
-        lower, upper, near = weights(c)
-        values = [ext[s, e, c].astype(jnp.float32) for e in range(count + 2 * reach)]
-        lefts = []
-        for b in range(branches):
-            mixed = []
-            for e in range(reach, reach + count):
-                below = jnp.where(near[b], values[e - 1], values[e - 2])
-                above = jnp.where(near[b], values[e + 1], values[e + 2])
-                mixed.append((lower[b] * below + upper[b] * above).astype(jnp.bfloat16))
-            lefts.append(jnp.dot(kbuf[s, b], jnp.concatenate(mixed, axis=1),
-                                 preferred_element_type=jnp.float32).astype(jnp.bfloat16))
-        rows = [jnp.concatenate([left[:, e * width:(e + 1) * width] for left in lefts], axis=1)
-                for e in range(count)]
-        return jnp.dot(jnp.concatenate(rows, axis=0), kt[s], preferred_element_type=jnp.float32)
+    def unit(blocks, s, c):
+        values = [blocks[e, c].astype(jnp.float32) for e in range(count + 2 * reach)]
+        return targets(values, kbuf.at[s], kt.at[s], *weights(c))
 
     def edge(c):
         lower, upper, near = weights(c)
         lefts = []
-        for s in range(2):
-            first = ext[s, reach + (count - 1) * outer, c].astype(jnp.float32)
-            second = ext[s, reach + 1 + (count - 3) * outer, c].astype(jnp.float32)
+        for s, blocks in enumerate((own, far)):
+            first = blocks[reach + (count - 1) * outer, c].astype(jnp.float32)
+            second = blocks[reach + 1 + (count - 3) * outer, c].astype(jnp.float32)
             for b in range(branches):
                 gain = jnp.where(outer == 0, upper[b], lower[b])
                 one = gain * jnp.where(near[b], first, second)
@@ -437,15 +454,8 @@
             edge_out[c, e] = sums[e * width:(e + 1) * width]
 
     def first_half(c, carry):
-        sums = unit(0, c)
-        for e in range(count):
-            acc[e, c] = sums[e * width:(e + 1) * width]
-
-        @pl.when(jnp.logical_and(has_outer, c > 0))
-        def _():
-            edge_copy(c - 1).start()
-
         x_copy(early, c).wait_recv()
+        release(c)
 
         @pl.when(has_outer)
         def _():
@@ -455,52 +465,70 @@
         def _():
             relay_copy(c).start()
 
+        sums = unit(own, 0, c)
+        for e in range(count):
+            acc[e, c] = sums[e]
+        pl.when(has_outer)(lambda: edge_copy(c).start())
         return carry
 
     lax.fori_loop(0, parts, first_half, 0)
 
-    def second_half(t, carry):
-        @pl.when(t < parts)
+    def arrived(c):
+        x_copy(late, c).wait_recv()
+        release(parts + c)
+        pl.when(has_outer)(lambda: relay_copy(c).start())
+
+    def halo(c):
+        relay_copy(c).wait_recv()
+
+        @pl.when(has_outer)
         def _():
-            x_copy(late, t).wait_recv()
-            pl.when(has_outer)(lambda: relay_copy(t).start())
-
-        @pl.when(jnp.logical_and(has_outer, t == 0))
-        def _():
-            edge_copy(parts - 1).start()
-
-        @pl.when(t > 0)
-        def _():
-            c = t - 1
-            relay_copy(c).wait_recv()
-            sums = unit(1, c)
-            for e in range(count):
-                acc[e, c] += sums[e * width:(e + 1) * width]
-
-            @pl.when(has_outer)
-            def _():
-                edge_copy(c).wait_recv()
-                acc[(count - 1) * outer, c] += edge_in[c, 0].astype(jnp.float32)
-                acc[1 + (count - 3) * outer, c] += edge_in[c, 1].astype(jnp.float32)
-
+            edge_copy(c).wait_recv()
+            acc[(count - 1) * outer, c] += edge_in[c, 0].astype(jnp.float32)
+            acc[1 + (count - 3) * outer, c] += edge_in[c, 1].astype(jnp.float32)
+
+    pl.when(has_outer)(lambda: arrived(0))
+
+    def second_half(c, carry):
+        pl.when(has_outer)(lambda: arrived(c + 1))
+        pl.when(jnp.logical_not(has_outer))(lambda: arrived(c))
+        halo(c)
+        sums = unit(far, 1, c)
+        for e in range(count):
+            acc[e, c] += sums[e]
         return carry
 
-    lax.fori_loop(0, parts + 1, second_half, 0)
+    lax.fori_loop(0, parts - 1, second_half, 0)
+    lower, upper, near = weights(parts - 1)
+    for b in range(branches):
+        for i, value in enumerate((lower[b], upper[b], jnp.where(near[b], 1.0, 0.0))):
+            scales[i, pl.ds(b, 1)] = jnp.full((1, width), value, jnp.float32)
+    pl.when(jnp.logical_not(has_outer))(lambda: arrived(parts - 1))
+    halo(parts - 1)
 
     def sent(ref, n):
         pltpu.make_async_copy(ref, ref, send.at[n]).wait()
 
-    sent(ext.at[1, pl.ds(reach, count)], 0)
-    sent(ext.at[0, pl.ds(0, reach)], 1)
-    sent(ext.at[1, pl.ds(0, reach)], 2)
+    sent(far.at[pl.ds(reach, count)], 0)
+    sent(own.at[pl.ds(0, reach)], 1)
+    sent(far.at[pl.ds(0, reach)], 2)
     pl.when(has_outer)(lambda: sent(edge_out, 3))
 
 
-def pair_write(sums, out, sem):
-    parts = sums.shape[1]
-    copies = [pltpu.make_async_copy(sums.at[:, c], out.at[:, 0, c], sem.at[c]) for c in range(parts)]
+def pair_finish(sums, far, kbuf, kt, scales, out, held, write, last_write):
+    count, parts = sums.shape[:2]
+    last = parts - 1
+    copies = [pltpu.make_async_copy(sums.at[:, c], out.at[:, 0, c], write.at[c]) for c in range(last)]
     for copy in copies:
         copy.start()
+    branches = range(kbuf.shape[1])
+    values = [far[e, last].astype(jnp.float32) for e in range(far.shape[0])]
+    rows = [[scales[i, pl.ds(b, 1)] for b in branches] for i in range(3)]
+    terms = targets(values, kbuf.at[1], kt.at[1], rows[0], rows[1], [row > 0.5 for row in rows[2]])
+    for e in range(count):
+        held[e] = sums[e, last] + terms[e]
+        copies.append(pltpu.make_async_copy(held.at[e], out.at[e, 0, last], last_write.at[e]))
+        copies[-1].start()
     for copy in copies:
         copy.wait()
 
@@ -511,17 +539,22 @@
     assert slices == 1 and count == 2 * OFFMAX
     dma = pltpu.SemaphoreType.DMA
     regular = pltpu.SemaphoreType.REGULAR
-    sums = pl.pallas_call(
+    vmem = pl.BlockSpec(memory_space=pltpu.VMEM)
+    made = pl.pallas_call(
         functools.partial(pair_kernel, n_energy),
-        out_shape=pltpu.VMEM((count, parts, width, width), jnp.float32),
+        out_shape=[
+            pltpu.VMEM((count, parts, width, width), jnp.float32),
+            pltpu.VMEM((count + 2 * OFFMAX, parts, width, width), jnp.bfloat16),
+            pltpu.VMEM((2, branches, width, width), jnp.bfloat16),
+            pltpu.VMEM((2, branches * width, width), jnp.bfloat16),
+            pltpu.VMEM((3, branches, width), jnp.float32),
+        ],
         in_specs=[pl.BlockSpec(memory_space=pl.ANY)] * 4,
-        out_specs=pl.BlockSpec(memory_space=pltpu.VMEM),
+        out_specs=[vmem] * 5,
         scratch_shapes=[
             pltpu.SMEM(offsets.shape, offsets.dtype),
             pltpu.SMEM(occupation.shape, occupation.dtype),
-            pltpu.VMEM((2, count + 2 * OFFMAX, parts, width, width), jnp.bfloat16),
-            pltpu.VMEM((2, branches, width, width), jnp.bfloat16),
-            pltpu.VMEM((2, branches * width, width), jnp.bfloat16),
+            pltpu.VMEM((count + 2 * OFFMAX, parts, width, width), jnp.bfloat16),
             pltpu.VMEM((parts, OFFMAX, width, width), jnp.bfloat16),
             pltpu.VMEM((parts, OFFMAX, width, width), jnp.bfloat16),
             dma((5,)),
@@ -536,12 +569,12 @@
         compiler_params=pltpu.CompilerParams(collective_id=0, has_side_effects=True),
     )(offsets, occupation, green, coupling)
     return pl.pallas_call(
-        pair_write,
+        pair_finish,
         out_shape=jax.ShapeDtypeStruct(green.shape, jnp.float32),
-        in_specs=[pl.BlockSpec(memory_space=pltpu.VMEM)],
+        in_specs=[vmem] * 5,
         out_specs=pl.BlockSpec(memory_space=pl.ANY),
-        scratch_shapes=[dma((parts,))],
-    )(pltpu.with_memory_space_constraint(sums, pltpu.VMEM))
+        scratch_shapes=[pltpu.VMEM((count, width, width), jnp.float32), dma((parts,)), dma((count,))],
+    )(*[pltpu.with_memory_space_constraint(x, pltpu.VMEM) for x in made])
 
 
 def solution(mesh):

time: 18.6 us -> 17.2 us (0.925)
  the two profiles are of different devices: /device:TPU:0 before, /device:TPU:31 now
where the time goes in v3:
time: 17.2 us; the launch traced here: 17.1 us
  Pallas kernels  17.1 us (99%)
    pallas_call x1, Pallas kernels, pair_body(): pl.pallas_call(functools.partial(pair_kernel, n_energy), out_shape=[pltpu...  15.8 us
    pallas_call x1, Pallas kernels, pair_body(): pl.pallas_call(pair_finish, out_shape=jax.ShapeDtypeStruct(green.shape, j...  1.26 us

profile of v3, /device:TPU:31, one launch (start us, length us, event | category | flops | bytes accessed | tf_op | source)
XLA Modules:
  0.0 17.1 jit_solution(14224025094200386772)
XLA Ops:
  0.0 15.8 %shard_map.46 = (f32[4,4,128,128]{3,2,1,0:T(8,128)S(1)}, bf16[8,4,128,128]{3,2,1,0:T(8,128)(2,1)S(1)}, bf16[2,4,128,128]{3,2,1,0:T(8,128)(2,1)S(1)}, bf16[2,512,128]{2,1,0:T(8,128)(2,1)S(1)}, f32[3,4,128]{2,1,0:T(4,128)S(1)}) custom-call(s32[4]{0:T(128)} %offsets_in.1, f32[4]{0:T(128)} %occupation_in.1, bf16[4,1,4,128,128]{4,3,2,1,0:T(8,128)(2,1)} %green.1, ...), custom_call_target="tpu_custom_call" | custom-call | tf_op jit(solution)/shard_map/pallas_call | solution.py:543
  15.8 1.3 %shard_map.47 = f32[4,1,4,128,128]{4,3,2,1,0:T(8,128)} custom-call(f32[4,4,128,128]{3,2,1,0:T(8,128)S(1)} %get-tuple-element.10.sums, bf16[8,4,128,128]{3,2,1,0:T(8,128)(2,1)S(1)} %get-tuple-element.11.far, bf16[2,4,128,128]{3,2,1,0:T(8,128)(2,1)S(1)} %get-tuple-element.12.kbuf, bf16[2,512,128]{2,1,0:T(8,128)(2,1)S(1)} %get-tuple-element.13.kt, ...), custom_call_target="tpu_custom_call" | custom-call | tf_op jit(solution)/shard_map/pallas_call | solution.py:571

commit v4 on v3

--- a/solution.py
+++ b/solution.py
@@ -373,7 +373,6 @@
         pl.semaphore_wait(reply_x, 1)
 
     held_back = jnp.logical_and(outer == 1, rank > 1)
-    longer = jnp.logical_and(cut == 0, has_outer)
     for c in range(parts):
         x_copy(early, c).start()
 
@@ -384,7 +383,7 @@
 
     def release(point):
         for c in range(parts):
-            at = jnp.where(longer, HOLD[0][c], HOLD[1][c])
+            at = jnp.where(cut == 0, HOLD[0][c], HOLD[1][c])
             pl.when(jnp.logical_and(held_back, point == at))(lambda: x_copy(late, c).start())
 
     local = [pltpu.make_async_copy(green.at[:, 0], own.at[pl.ds(reach, count)], local_sem.at[0]),

time: 17.2 us -> 16.9 us (0.983)
  the two profiles are of different devices: /device:TPU:31 before, /device:TPU:0 now
where the time goes in v4:
time: 16.9 us; the launch traced here: 16.6 us
  Pallas kernels  16.6 us (98%)
    pallas_call x1, Pallas kernels, pair_body(): pl.pallas_call(functools.partial(pair_kernel, n_energy), out_shape=[pltpu...  15.4 us
    pallas_call x1, Pallas kernels, pair_body(): pl.pallas_call(pair_finish, out_shape=jax.ShapeDtypeStruct(green.shape, j...  1.26 us

profile of v4, /device:TPU:0, one launch (start us, length us, event | category | flops | bytes accessed | tf_op | source)
XLA Modules:
  0.0 16.6 jit_solution(2691864622722952510)
XLA Ops:
  0.0 15.4 %shard_map.46 = (f32[4,4,128,128]{3,2,1,0:T(8,128)S(1)}, bf16[8,4,128,128]{3,2,1,0:T(8,128)(2,1)S(1)}, bf16[2,4,128,128]{3,2,1,0:T(8,128)(2,1)S(1)}, bf16[2,512,128]{2,1,0:T(8,128)(2,1)S(1)}, f32[3,4,128]{2,1,0:T(4,128)S(1)}) custom-call(s32[4]{0:T(128)} %offsets_in.1, f32[4]{0:T(128)} %occupation_in.1, bf16[4,1,4,128,128]{4,3,2,1,0:T(8,128)(2,1)} %green.1, ...), custom_call_target="tpu_custom_call" | custom-call | tf_op jit(solution)/shard_map/pallas_call | solution.py:542
  15.4 1.3 %shard_map.47 = f32[4,1,4,128,128]{4,3,2,1,0:T(8,128)} custom-call(f32[4,4,128,128]{3,2,1,0:T(8,128)S(1)} %get-tuple-element.10.sums, bf16[8,4,128,128]{3,2,1,0:T(8,128)(2,1)S(1)} %get-tuple-element.11.far, bf16[2,4,128,128]{3,2,1,0:T(8,128)(2,1)S(1)} %get-tuple-element.12.kbuf, bf16[2,512,128]{2,1,0:T(8,128)(2,1)S(1)} %get-tuple-element.13.kt, ...), custom_call_target="tpu_custom_call" | custom-call | tf_op jit(solution)/shard_map/pallas_call | solution.py:570

commit v5 on v4

--- a/solution.py
+++ b/solution.py
@@ -7,7 +7,7 @@
 from jax.sharding import PartitionSpec as P
 
 OFFMAX = 2
-HOLD = ((3, 3, 4, 4), (2, 2, 3, 3))
+HOLD = ((3, 3, 4, 5), (2, 2, 3, 3))
 MESH = pl.DeviceIdType.MESH
 
 
@@ -305,7 +305,7 @@
     cut = lax.axis_index("cuts")
     reach = OFFMAX
     count, parts, width = own.shape[0] - 2 * reach, own.shape[1], own.shape[2]
-    branches = kbuf.shape[1]
+    branches, half = kbuf.shape[1], count // 2
     outer = rank % 2
     inner = 1 - outer
     has_outer = jnp.where(outer == 0, rank, n_energy - 1 - rank) > 0
@@ -334,17 +334,17 @@
     def own_copy():
         return pltpu.make_async_remote_copy(
             src_ref=green.at[edge_at(inner), 0], dst_ref=own.at[halo_at(outer)],
-            send_sem=send.at[1], recv_sem=own_recv, device_id=core_peer, device_id_type=MESH)
+            send_sem=send.at[0], recv_sem=own_recv, device_id=core_peer, device_id_type=MESH)
 
     def relay_copy(c):
         return pltpu.make_async_remote_copy(
             src_ref=far.at[own_at(inner), c], dst_ref=far.at[halo_at(outer), c],
-            send_sem=send.at[2], recv_sem=relay_recv.at[c], device_id=core_peer, device_id_type=MESH)
+            send_sem=send.at[0], recv_sem=relay_recv.at[c], device_id=core_peer, device_id_type=MESH)
 
     def edge_copy(c):
         return pltpu.make_async_remote_copy(
             src_ref=edge_out.at[c], dst_ref=edge_in.at[c],
-            send_sem=send.at[3], recv_sem=edge_recv.at[c], device_id=chip_peer, device_id_type=MESH)
+            send_sem=send.at[1], recv_sem=edge_recv, device_id=chip_peer, device_id_type=MESH)
 
     def signal(sem, device):
         pl.semaphore_signal(sem, inc=1, device_id=device, device_id_type=MESH)
@@ -387,12 +387,15 @@
             pl.when(jnp.logical_and(held_back, point == at))(lambda: x_copy(late, c).start())
 
     local = [pltpu.make_async_copy(green.at[:, 0], own.at[pl.ds(reach, count)], local_sem.at[0]),
-             pltpu.make_async_copy(coupling.at[:, 1, 0], kbuf.at[0], local_sem.at[1]),
-             pltpu.make_async_copy(coupling.at[:, 2 - 2 * cut, 0], kbuf.at[1], local_sem.at[2]),
-             pltpu.make_async_copy(offsets_in, offsets, local_sem.at[3]),
-             pltpu.make_async_copy(occupation_in, occupation, local_sem.at[4])]
+             pltpu.make_async_copy(offsets_in, offsets, local_sem.at[1]),
+             pltpu.make_async_copy(occupation_in, occupation, local_sem.at[2])]
     for copy in local:
         copy.start()
+    pltpu.make_async_copy(coupling.at[:, 1, 0], kbuf.at[0], local_sem.at[3]).start()
+    pltpu.make_async_copy(coupling.at[:, 2 - 2 * cut, 0], kbuf.at[1], local_sem.at[3]).start()
+
+    def whole(ref, sem):
+        pltpu.make_async_copy(ref, ref, sem).wait()
 
     @pl.when(tells)
     def _():
@@ -411,6 +414,7 @@
 
     own[halo_at(outer)] = jnp.zeros((reach, parts, width, width), own.dtype)
     far[halo_at(outer)] = jnp.zeros((reach, parts, width, width), far.dtype)
+    whole(kbuf, local_sem.at[3])
     for copy in local:
         copy.wait()
     for s in range(2):
@@ -429,8 +433,8 @@
         upper = [jnp.where(lesser, occupation[b] + 1.0, occupation[b]) for b in range(branches)]
         return lower, upper, [offsets[b] == 1 for b in range(branches)]
 
-    def unit(blocks, s, c):
-        values = [blocks[e, c].astype(jnp.float32) for e in range(count + 2 * reach)]
+    def unit(blocks, s, c, start=0, n=count):
+        values = [blocks[start + e, c].astype(jnp.float32) for e in range(n + 2 * reach)]
         return targets(values, kbuf.at[s], kt.at[s], *weights(c))
 
     def edge(c):
@@ -477,59 +481,81 @@
         release(parts + c)
         pl.when(has_outer)(lambda: relay_copy(c).start())
 
-    def halo(c):
-        relay_copy(c).wait_recv()
-
-        @pl.when(has_outer)
-        def _():
-            edge_copy(c).wait_recv()
-            acc[(count - 1) * outer, c] += edge_in[c, 0].astype(jnp.float32)
-            acc[1 + (count - 3) * outer, c] += edge_in[c, 1].astype(jnp.float32)
+    def add(jobs):
+        for (c, start, n), made in zip(jobs, [unit(far, 1, *job) for job in jobs]):
+            for e in range(n):
+                acc[start + e, c] += made[e]
 
     pl.when(has_outer)(lambda: arrived(0))
 
     def second_half(c, carry):
         pl.when(has_outer)(lambda: arrived(c + 1))
         pl.when(jnp.logical_not(has_outer))(lambda: arrived(c))
-        halo(c)
-        sums = unit(far, 1, c)
-        for e in range(count):
-            acc[e, c] += sums[e]
+        relay_copy(c).wait_recv()
+        add([(c, 0, count)])
         return carry
 
-    lax.fori_loop(0, parts - 1, second_half, 0)
-    lower, upper, near = weights(parts - 1)
+    lax.fori_loop(0, parts - 2, second_half, 0)
+    last = parts - 1
+    lower, upper, near = weights(last)
     for b in range(branches):
         for i, value in enumerate((lower[b], upper[b], jnp.where(near[b], 1.0, 0.0))):
             scales[i, pl.ds(b, 1)] = jnp.full((1, width), value, jnp.float32)
-    pl.when(jnp.logical_not(has_outer))(lambda: arrived(parts - 1))
-    halo(parts - 1)
-
-    def sent(ref, n):
-        pltpu.make_async_copy(ref, ref, send.at[n]).wait()
-
-    sent(far.at[pl.ds(reach, count)], 0)
-    sent(own.at[pl.ds(0, reach)], 1)
-    sent(far.at[pl.ds(0, reach)], 2)
-    pl.when(has_outer)(lambda: sent(edge_out, 3))
-
-
-def pair_finish(sums, far, kbuf, kt, scales, out, held, write, last_write):
+    c = last - 1
+
+    @pl.when(has_outer)
+    def _():
+        arrived(last)
+        relay_copy(c).wait_recv()
+        add([(c, 0, count), (last, half * outer, half)])
+
+    @pl.when(jnp.logical_not(has_outer))
+    def _():
+        arrived(c)
+        relay_copy(c).wait_recv()
+        add([(c, 0, count)])
+
+    @pl.when(has_outer)
+    def _():
+        whole(edge_in, edge_recv)
+        for c in range(parts):
+            acc[(count - 1) * outer, c] += edge_in[c, 0].astype(jnp.float32)
+            acc[1 + (count - 3) * outer, c] += edge_in[c, 1].astype(jnp.float32)
+
+    pl.when(jnp.logical_not(has_outer))(lambda: arrived(last))
+    relay_copy(last).wait_recv()
+    whole(own, send.at[0])
+    pl.when(has_outer)(lambda: whole(edge_out, send.at[1]))
+
+
+def pair_finish(n_energy, sums, far, kbuf, kt, scales, out, held, sem):
+    rank = lax.axis_index("energy")
     count, parts = sums.shape[:2]
-    last = parts - 1
-    copies = [pltpu.make_async_copy(sums.at[:, c], out.at[:, 0, c], write.at[c]) for c in range(last)]
-    for copy in copies:
-        copy.start()
-    branches = range(kbuf.shape[1])
-    values = [far[e, last].astype(jnp.float32) for e in range(far.shape[0])]
-    rows = [[scales[i, pl.ds(b, 1)] for b in branches] for i in range(3)]
-    terms = targets(values, kbuf.at[1], kt.at[1], rows[0], rows[1], [row > 0.5 for row in rows[2]])
-    for e in range(count):
-        held[e] = sums[e, last] + terms[e]
-        copies.append(pltpu.make_async_copy(held.at[e], out.at[e, 0, last], last_write.at[e]))
-        copies[-1].start()
-    for copy in copies:
-        copy.wait()
+    last, half = parts - 1, count // 2
+    outer = rank % 2
+    has_outer = jnp.where(outer == 0, rank, n_energy - 1 - rank) > 0
+
+    def write(source, start, n, c):
+        pltpu.make_async_copy(source, out.at[pl.ds(start, n), 0, c], sem).start()
+
+    for c in range(last):
+        write(sums.at[:, c], 0, count, c)
+
+    def add(start, n):
+        values = [far[start + e, last].astype(jnp.float32) for e in range(n + 2 * OFFMAX)]
+        rows = [[scales[i, pl.ds(b, 1)] for b in range(kbuf.shape[1])] for i in range(3)]
+        made = targets(values, kbuf.at[1], kt.at[1], rows[0], rows[1], [row > 0.5 for row in rows[2]])
+        for e in range(n):
+            held[e] = sums[start + e, last] + made[e]
+            write(held.at[pl.ds(e, 1)], start + e, 1, last)
+
+    @pl.when(has_outer)
+    def _():
+        write(sums.at[pl.ds(half * outer, half), last], half * outer, half, last)
+        add(half * (1 - outer), half)
+
+    pl.when(jnp.logical_not(has_outer))(lambda: add(0, count))
+    pltpu.make_async_copy(sums, sums, sem).wait()
 
 
 def pair_body(n_energy, green, offsets, occupation, coupling):
@@ -556,23 +582,23 @@
             pltpu.VMEM((count + 2 * OFFMAX, parts, width, width), jnp.bfloat16),
             pltpu.VMEM((parts, OFFMAX, width, width), jnp.bfloat16),
             pltpu.VMEM((parts, OFFMAX, width, width), jnp.bfloat16),
-            dma((5,)),
+            dma((4,)),
             regular,
             regular((2,)),
-            dma((4,)),
+            dma((2,)),
             dma((2, parts)),
             dma,
             dma((parts,)),
-            dma((parts,)),
+            dma,
         ],
         compiler_params=pltpu.CompilerParams(collective_id=0, has_side_effects=True),
     )(offsets, occupation, green, coupling)
     return pl.pallas_call(
-        pair_finish,
+        functools.partial(pair_finish, n_energy),
         out_shape=jax.ShapeDtypeStruct(green.shape, jnp.float32),
         in_specs=[vmem] * 5,
         out_specs=pl.BlockSpec(memory_space=pl.ANY),
-        scratch_shapes=[pltpu.VMEM((count, width, width), jnp.float32), dma((parts,)), dma((count,))],
+        scratch_shapes=[pltpu.VMEM((count, width, width), jnp.float32), dma],
     )(*[pltpu.with_memory_space_constraint(x, pltpu.VMEM) for x in made])
 
 

time: 16.9 us -> 16.7 us (0.988)
  no operation moved by 1% of the time
where the time goes in v5:
time: 16.7 us; the launch traced here: 16.5 us
  Pallas kernels  16.5 us (99%)
    pallas_call x1, Pallas kernels, pair_body(): pl.pallas_call(functools.partial(pair_kernel, n_energy), out_shape=[pltpu...  15.3 us
    pallas_call x1, Pallas kernels, pair_body(): pl.pallas_call(functools.partial(pair_finish, n_energy), out_shape=jax.Sh...  1.22 us

profile of v5, /device:TPU:0, one launch (start us, length us, event | category | flops | bytes accessed | tf_op | source)
XLA Modules:
  0.0 16.5 jit_solution(16824907210084883687)
XLA Ops:
  0.0 15.3 %shard_map.46 = (f32[4,4,128,128]{3,2,1,0:T(8,128)S(1)}, bf16[8,4,128,128]{3,2,1,0:T(8,128)(2,1)S(1)}, bf16[2,4,128,128]{3,2,1,0:T(8,128)(2,1)S(1)}, bf16[2,512,128]{2,1,0:T(8,128)(2,1)S(1)}, f32[3,4,128]{2,1,0:T(4,128)S(1)}) custom-call(s32[4]{0:T(128)} %offsets_in.1, f32[4]{0:T(128)} %occupation_in.1, bf16[4,1,4,128,128]{4,3,2,1,0:T(8,128)(2,1)} %green.1, ...), custom_call_target="tpu_custom_call" | custom-call | tf_op jit(solution)/shard_map/pallas_call | solution.py:568
  15.3 1.2 %shard_map.47 = f32[4,1,4,128,128]{4,3,2,1,0:T(8,128)} custom-call(f32[4,4,128,128]{3,2,1,0:T(8,128)S(1)} %get-tuple-element.10.sums, bf16[8,4,128,128]{3,2,1,0:T(8,128)(2,1)S(1)} %get-tuple-element.11.far, bf16[2,4,128,128]{3,2,1,0:T(8,128)(2,1)S(1)} %get-tuple-element.12.kbuf, bf16[2,512,128]{2,1,0:T(8,128)(2,1)S(1)} %get-tuple-element.13.kt, ...), custom_call_target="tpu_custom_call" | custom-call | tf_op jit(solution)/shard_map/pallas_call | solution.py:596

commit v6 on v5

--- a/solution.py
+++ b/solution.py
@@ -355,11 +355,11 @@
     def _():
         signal(barrier, slice_peer)
 
-    @pl.when(told)
+    @pl.when(jnp.logical_and(told, cut == 0))
     def _():
         signal(barrier, core_peer)
 
-    @pl.when(jnp.logical_and(told, has_outer))
+    @pl.when(jnp.logical_and(jnp.logical_and(told, cut == 0), has_outer))
     def _():
         signal(barrier, chip_peer)
 
@@ -375,6 +375,14 @@
     held_back = jnp.logical_and(outer == 1, rank > 1)
     for c in range(parts):
         x_copy(early, c).start()
+
+    @pl.when(jnp.logical_and(told, cut != 0))
+    def _():
+        signal(barrier, core_peer)
+
+    @pl.when(jnp.logical_and(jnp.logical_and(told, cut != 0), has_outer))
+    def _():
+        signal(barrier, chip_peer)
 
     @pl.when(jnp.logical_not(held_back))
     def _():
@@ -386,13 +394,13 @@
             at = jnp.where(cut == 0, HOLD[0][c], HOLD[1][c])
             pl.when(jnp.logical_and(held_back, point == at))(lambda: x_copy(late, c).start())
 
-    local = [pltpu.make_async_copy(green.at[:, 0], own.at[pl.ds(reach, count)], local_sem.at[0]),
-             pltpu.make_async_copy(offsets_in, offsets, local_sem.at[1]),
+    loads = [pltpu.make_async_copy(green.at[:, 0], own.at[pl.ds(reach, count)], local_sem.at[0]),
+             pltpu.make_async_copy(coupling.at[:, 1, 0], kbuf.at[0], local_sem.at[0]),
+             pltpu.make_async_copy(coupling.at[:, 2 - 2 * cut, 0], kbuf.at[1], local_sem.at[0])]
+    local = [pltpu.make_async_copy(offsets_in, offsets, local_sem.at[1]),
              pltpu.make_async_copy(occupation_in, occupation, local_sem.at[2])]
-    for copy in local:
+    for copy in loads + local:
         copy.start()
-    pltpu.make_async_copy(coupling.at[:, 1, 0], kbuf.at[0], local_sem.at[3]).start()
-    pltpu.make_async_copy(coupling.at[:, 2 - 2 * cut, 0], kbuf.at[1], local_sem.at[3]).start()
 
     def whole(ref, sem):
         pltpu.make_async_copy(ref, ref, sem).wait()
@@ -414,7 +422,7 @@
 
     own[halo_at(outer)] = jnp.zeros((reach, parts, width, width), own.dtype)
     far[halo_at(outer)] = jnp.zeros((reach, parts, width, width), far.dtype)
-    whole(kbuf, local_sem.at[3])
+    whole(own.at[pl.ds(0, count + 2 * branches // parts)], local_sem.at[0])
     for copy in local:
         copy.wait()
     for s in range(2):
@@ -562,6 +570,7 @@
     count, slices, parts, width, _ = green.shape
     branches = coupling.shape[0]
     assert slices == 1 and count == 2 * OFFMAX
+    assert 2 * branches % parts == 0 and 2 * branches <= 2 * OFFMAX * parts
     dma = pltpu.SemaphoreType.DMA
     regular = pltpu.SemaphoreType.REGULAR
     vmem = pl.BlockSpec(memory_space=pltpu.VMEM)
@@ -582,7 +591,7 @@
             pltpu.VMEM((count + 2 * OFFMAX, parts, width, width), jnp.bfloat16),
             pltpu.VMEM((parts, OFFMAX, width, width), jnp.bfloat16),
             pltpu.VMEM((parts, OFFMAX, width, width), jnp.bfloat16),
-            dma((4,)),
+            dma((3,)),
             regular,
             regular((2,)),
             dma((2,)),

time: 16.7 us -> 16.7 us (level)
  no operation moved by 1% of the time
where the time goes in v6:
time: 16.7 us; the launch traced here: 16.5 us
  Pallas kernels  16.5 us (99%)
    pallas_call x1, Pallas kernels, pair_body(): pl.pallas_call(functools.partial(pair_kernel, n_energy), out_shape=[pltpu...  15.3 us
    pallas_call x1, Pallas kernels, pair_body(): pl.pallas_call(functools.partial(pair_finish, n_energy), out_shape=jax.Sh...  1.22 us

profile of v6, /device:TPU:0, one launch (start us, length us, event | category | flops | bytes accessed | tf_op | source)
XLA Modules:
  0.0 16.5 jit_solution(10407899732445266312)
XLA Ops:
  0.0 15.3 %shard_map.46 = (f32[4,4,128,128]{3,2,1,0:T(8,128)S(1)}, bf16[8,4,128,128]{3,2,1,0:T(8,128)(2,1)S(1)}, bf16[2,4,128,128]{3,2,1,0:T(8,128)(2,1)S(1)}, bf16[2,512,128]{2,1,0:T(8,128)(2,1)S(1)}, f32[3,4,128]{2,1,0:T(4,128)S(1)}) custom-call(s32[4]{0:T(128)} %offsets_in.1, f32[4]{0:T(128)} %occupation_in.1, bf16[4,1,4,128,128]{4,3,2,1,0:T(8,128)(2,1)} %green.1, ...), custom_call_target="tpu_custom_call" | custom-call | tf_op jit(solution)/shard_map/pallas_call | solution.py:577
  15.3 1.2 %shard_map.47 = f32[4,1,4,128,128]{4,3,2,1,0:T(8,128)} custom-call(f32[4,4,128,128]{3,2,1,0:T(8,128)S(1)} %get-tuple-element.10.sums, bf16[8,4,128,128]{3,2,1,0:T(8,128)(2,1)S(1)} %get-tuple-element.11.far, bf16[2,4,128,128]{3,2,1,0:T(8,128)(2,1)S(1)} %get-tuple-element.12.kbuf, bf16[2,512,128]{2,1,0:T(8,128)(2,1)S(1)} %get-tuple-element.13.kt, ...), custom_call_target="tpu_custom_call" | custom-call | tf_op jit(solution)/shard_map/pallas_call | solution.py:605

commit v7 on v6

--- a/solution.py
+++ b/solution.py
@@ -355,11 +355,11 @@
     def _():
         signal(barrier, slice_peer)
 
-    @pl.when(jnp.logical_and(told, cut == 0))
+    @pl.when(told)
     def _():
         signal(barrier, core_peer)
 
-    @pl.when(jnp.logical_and(jnp.logical_and(told, cut == 0), has_outer))
+    @pl.when(jnp.logical_and(told, has_outer))
     def _():
         signal(barrier, chip_peer)
 
@@ -375,14 +375,6 @@
     held_back = jnp.logical_and(outer == 1, rank > 1)
     for c in range(parts):
         x_copy(early, c).start()
-
-    @pl.when(jnp.logical_and(told, cut != 0))
-    def _():
-        signal(barrier, core_peer)
-
-    @pl.when(jnp.logical_and(jnp.logical_and(told, cut != 0), has_outer))
-    def _():
-        signal(barrier, chip_peer)
 
     @pl.when(jnp.logical_not(held_back))
     def _():
@@ -546,8 +538,7 @@
     def write(source, start, n, c):
         pltpu.make_async_copy(source, out.at[pl.ds(start, n), 0, c], sem).start()
 
-    for c in range(last):
-        write(sums.at[:, c], 0, count, c)
+    write(sums.at[:, pl.ds(0, last)], 0, count, pl.ds(0, last))
 
     def add(start, n):
         values = [far[start + e, last].astype(jnp.float32) for e in range(n + 2 * OFFMAX)]

time: 16.7 us -> 16.7 us (level)
  no operation moved by 1% of the time
where the time goes in v7:
time: 16.7 us; the launch traced here: 16.5 us
  Pallas kernels  16.5 us (99%)
    pallas_call x1, Pallas kernels, pair_body(): pl.pallas_call(functools.partial(pair_kernel, n_energy), out_shape=[pltpu...  15.3 us
    pallas_call x1, Pallas kernels, pair_body(): pl.pallas_call(functools.partial(pair_finish, n_energy), out_shape=jax.Sh...  1.22 us

profile of v7, /device:TPU:0, one launch (start us, length us, event | category | flops | bytes accessed | tf_op | source)
XLA Modules:
  0.0 16.5 jit_solution(9424502537921962214)
XLA Ops:
  0.0 15.3 %shard_map.46 = (f32[4,4,128,128]{3,2,1,0:T(8,128)S(1)}, bf16[8,4,128,128]{3,2,1,0:T(8,128)(2,1)S(1)}, bf16[2,4,128,128]{3,2,1,0:T(8,128)(2,1)S(1)}, bf16[2,512,128]{2,1,0:T(8,128)(2,1)S(1)}, f32[3,4,128]{2,1,0:T(4,128)S(1)}) custom-call(s32[4]{0:T(128)} %offsets_in.1, f32[4]{0:T(128)} %occupation_in.1, bf16[4,1,4,128,128]{4,3,2,1,0:T(8,128)(2,1)} %green.1, ...), custom_call_target="tpu_custom_call" | custom-call | tf_op jit(solution)/shard_map/pallas_call | solution.py:568
  15.3 1.2 %shard_map.47 = f32[4,1,4,128,128]{4,3,2,1,0:T(8,128)} custom-call(f32[4,4,128,128]{3,2,1,0:T(8,128)S(1)} %get-tuple-element.10.sums, bf16[8,4,128,128]{3,2,1,0:T(8,128)(2,1)S(1)} %get-tuple-element.11.far, bf16[2,4,128,128]{3,2,1,0:T(8,128)(2,1)S(1)} %get-tuple-element.12.kbuf, bf16[2,512,128]{2,1,0:T(8,128)(2,1)S(1)} %get-tuple-element.13.kt, ...), custom_call_target="tpu_custom_call" | custom-call | tf_op jit(solution)/shard_map/pallas_call | solution.py:596

commit v8 on v5

--- a/solution.py
+++ b/solution.py
@@ -7,7 +7,7 @@
 from jax.sharding import PartitionSpec as P
 
 OFFMAX = 2
-HOLD = ((3, 3, 4, 5), (2, 2, 3, 3))
+HOLD = ((3, 3, 4, 5), (2, 3, 3, 3))
 MESH = pl.DeviceIdType.MESH
 
 

time: 16.7 us -> 16.7 us (level)
  no operation moved by 1% of the time
where the time goes in v8:
time: 16.7 us; the launch traced here: 16.5 us
  Pallas kernels  16.5 us (99%)
    pallas_call x1, Pallas kernels, pair_body(): pl.pallas_call(functools.partial(pair_kernel, n_energy), out_shape=[pltpu...  15.3 us
    pallas_call x1, Pallas kernels, pair_body(): pl.pallas_call(functools.partial(pair_finish, n_energy), out_shape=jax.Sh...  1.22 us

profile of v8, /device:TPU:0, one launch (start us, length us, event | category | flops | bytes accessed | tf_op | source)
XLA Modules:
  0.0 16.5 jit_solution(8453103945299397937)
XLA Ops:
  0.0 15.3 %shard_map.46 = (f32[4,4,128,128]{3,2,1,0:T(8,128)S(1)}, bf16[8,4,128,128]{3,2,1,0:T(8,128)(2,1)S(1)}, bf16[2,4,128,128]{3,2,1,0:T(8,128)(2,1)S(1)}, bf16[2,512,128]{2,1,0:T(8,128)(2,1)S(1)}, f32[3,4,128]{2,1,0:T(4,128)S(1)}) custom-call(s32[4]{0:T(128)} %offsets_in.1, f32[4]{0:T(128)} %occupation_in.1, bf16[4,1,4,128,128]{4,3,2,1,0:T(8,128)(2,1)} %green.1, ...), custom_call_target="tpu_custom_call" | custom-call | tf_op jit(solution)/shard_map/pallas_call | solution.py:568
  15.3 1.2 %shard_map.47 = f32[4,1,4,128,128]{4,3,2,1,0:T(8,128)} custom-call(f32[4,4,128,128]{3,2,1,0:T(8,128)S(1)} %get-tuple-element.10.sums, bf16[8,4,128,128]{3,2,1,0:T(8,128)(2,1)S(1)} %get-tuple-element.11.far, bf16[2,4,128,128]{3,2,1,0:T(8,128)(2,1)S(1)} %get-tuple-element.12.kbuf, bf16[2,512,128]{2,1,0:T(8,128)(2,1)S(1)} %get-tuple-element.13.kt, ...), custom_call_target="tpu_custom_call" | custom-call | tf_op jit(solution)/shard_map/pallas_call | solution.py:596
